TPU v7x, 128 devices: a whole 4x4x4 slice. The times are simulated.
128 devices in a mesh: dp: 64 (over z, y, x), mp: 2 (over core).
Axes of the slice: x: 4, y: 4, z: 4, core: 2. Of those that a mesh axis runs over, the one named last changes fastest.
Arguments:
- pixels: bfloat16 [128, 512, 768], P(('dp', 'mp')), may hold values from -6 to 6
- counts: int32 [64, 2], P('dp'), may hold values from 128 to 512
- owner: int32 [64, 2], P('dp'), may hold values from 0 to 1, each once within a row
- embed_weight: bfloat16 [768, 1024], P('dp', 'mp'), may hold values from -0.21875 to 0.21875
- w_qkv: bfloat16 [3, 1024, 1024], P(None, 'dp', 'mp'), may hold values from -0.8 to 0.8
- w_out: bfloat16 [1024, 1024], P('mp', 'dp'), may hold values from -0.1875 to 0.1875
- w_up: bfloat16 [1024, 4096], P('dp', 'mp'), may hold values from -0.1875 to 0.1875
- w_down: bfloat16 [4096, 1024], P('mp', 'dp'), may hold values from -0.09375 to 0.09375
- ln1_gain: float32 [1024], replicated, may hold values from 0.25 to 1.75
- ln2_gain: float32 [1024], replicated, may hold values from 0.25 to 1.75
- targets: bfloat16 [64, 2, 512, 1024], P('dp', None, 'mp'), may hold values from -20 to 20
Outputs:
- encoded: bfloat16 [64, 2, 512, 1024], P('dp', None, 'mp')
- mean_loss: float32 [], replicated
Inputs may be any that keep to these rules, and one draw needn't show every extreme that they name: counts[g, r] is the number of valid patches at the start of image g * 2 + r; the remaining patch slots are padding. Each row owner[g, :] is a permutation of 0 to 2 - 1, so every held image is encoded once.
All inputs are finite; a program needn't handle non-finite values.
Results may differ from a plain program's by a relative error of at most 0.014.
Values may be sent and summed in bfloat16 or wider, within the bound.
A program may use at most 128 MiB of HBM per device.

v0:
```python
import jax
import jax.numpy as jnp
from jax import lax
from jax.sharding import Mesh
from jax.sharding import PartitionSpec as P

D = 1024
HEAD = 64
DP = ("dp_0", "dp_1", "dp_2")
DP_MP = ("dp_0", "dp_1", "dp_2", "mp")


def joined_along(tiles, dim):
    dims = list(tiles.shape[1:])
    dims[dim] *= tiles.shape[0]
    return jnp.moveaxis(tiles, 0, dim).reshape(dims)


def one_gather(arrays, axis, dims):
    line = jnp.concatenate([a.reshape(-1) for a in arrays])
    lines, at, finished = (lax.all_gather(line, axis), 0, [])
    for a, dim in zip(arrays, dims):
        tiles = lines[:, at : at + a.size].reshape(-1, *a.shape)
        finished.append(joined_along(tiles, dim))
        at += a.size
    return tuple(finished)


def rows_first(arrays, axis, dims):
    turned = [jnp.moveaxis(a, dim, 0) for a, dim in zip(arrays, dims)]
    both = jnp.concatenate([t.reshape(len(t), -1) for t in turned], axis=1)
    whole, at, finished = (lax.all_gather(both, axis, axis=0, tiled=True), 0, [])
    for t, dim in zip(turned, dims):
        section = whole[:, at : at + t[0].size].reshape(-1, *t.shape[1:])
        finished.append(jnp.moveaxis(section, 0, dim))
        at += t[0].size
    return tuple(finished)


def broadcast(shard, axis, root):
    return lax.dynamic_index_in_dim(lax.all_gather(shard, axis), root, 0, keepdims=False)


def copy_for_each(shard, axis):
    length = lax.axis_size(axis)
    return lax.all_to_all(
        jnp.broadcast_to(shard[None], (length, *shard.shape)), axis, 0, 0, tiled=True
    )


def gathered_copies(shard, axis, dim):
    return joined_along(copy_for_each(shard, axis), dim)


def cut_along(shard, dim, length):
    before, after = (shard.shape[:dim], shard.shape[dim + 1 :])
    return jnp.moveaxis(shard.reshape(*before, length, -1, *after), dim, 0)


def sent_and_summed(shard, axis, dim):
    length = lax.axis_size(axis)
    tiles = lax.all_to_all(cut_along(shard, dim, length), axis, 0, 0, tiled=True)
    return jnp.sum(tiles.astype(jnp.float32), axis=0)


def by_axis(shard, axes):
    for axis in axes:
        shard = lax.psum(shard, axis)
    return shard


def layer_norm(inputs, gains):
    average = jnp.mean(inputs, axis=-1, keepdims=True)
    centred = inputs - average
    spread = jnp.mean(centred * centred, axis=-1, keepdims=True)
    return centred * lax.rsqrt(spread + 1e-06) * gains


def attend(queries, key_rows, value_rows, usable):

    def one_head(operands):
        query_part, key_part, value_part = operands
        scores = jnp.einsum("qd,kd->qk", query_part, key_part, preferred_element_type=jnp.float32)
        scores = jnp.where(usable[None, :], scores, -1e30)
        row_max = jnp.max(scores, axis=-1, keepdims=True)
        expo = jnp.exp(scores - row_max)
        row_sum = jnp.sum(expo, axis=-1)
        mixed = jnp.dot(expo.astype(jnp.bfloat16), value_part, preferred_element_type=jnp.float32)
        return mixed / row_sum[:, None]

    return lax.map(one_head, (queries, key_rows, value_rows))


def attention_heads(queries, key_rows, value_rows, length, patches):
    usable = jnp.arange(patches, dtype=jnp.int32) < length
    quarter = patches // 4

    def limited(extent):

        def branch_fn():
            return attend(queries, key_rows[:, :extent], value_rows[:, :extent], usable[:extent])

        return branch_fn

    return lax.switch(
        (length - 1) // quarter, [limited(quarter * (blocks_used + 1)) for blocks_used in range(4)]
    )


def split_heads(projected, patches, factor):
    width = projected.shape[2]
    heads_here = width // HEAD
    queries = (
        (projected[0] * factor)
        .astype(jnp.bfloat16)
        .reshape(patches, heads_here, HEAD)
        .transpose(1, 0, 2)
    )
    key_rows = (
        projected[1].astype(jnp.bfloat16).reshape(patches, heads_here, HEAD).transpose(1, 0, 2)
    )
    value_rows = (
        projected[2].astype(jnp.bfloat16).reshape(patches, heads_here, HEAD).transpose(1, 0, 2)
    )
    return (queries, key_rows, value_rows)


def on_device(
    pixels, counts, owner, embed_weight, w_qkv, w_out, w_up, w_down, ln1_gain, ln2_gain, targets
):
    picture = pixels[0]
    patches = picture.shape[0]
    group_size = lax.axis_size("mp")
    position = lax.axis_index("mp")
    rows_own = patches // group_size
    order = owner[0]
    lengths_all = counts[0]
    slot_ids = jnp.arange(group_size, dtype=jnp.int32)
    factor = HEAD ** (-0.5)
    embed_cols, up_cols = one_gather((embed_weight, w_up), DP, (0, 0))
    qkv_cols, out_rows, down_rows = rows_first((w_qkv, w_out, w_down), DP, (1, 1, 1))

    def step(slot, carry):
        stored, squares_run, number_run = carry
        root = order[slot]
        length = jnp.sum(jnp.where(slot_ids == root, lengths_all, 0))
        shared = broadcast(picture, "mp", root)
        slab = jnp.dot(shared, embed_cols, preferred_element_type=jnp.float32).astype(jnp.bfloat16)
        tokens = gathered_copies(slab, "mp", 1)
        normed = layer_norm(tokens.astype(jnp.float32), ln1_gain).astype(jnp.bfloat16)
        projected = jnp.einsum("pd,cdh->cph", normed, qkv_cols, preferred_element_type=jnp.float32)
        queries, key_rows, value_rows = split_heads(projected, patches, factor)
        mixture = attention_heads(queries, key_rows, value_rows, length, patches)
        attended = (
            mixture.transpose(1, 0, 2).astype(jnp.bfloat16).reshape(patches, qkv_cols.shape[2])
        )
        attention_rows = sent_and_summed(
            jnp.dot(
                lax.slice_in_dim(attended, 0, rows_own * lax.axis_size("mp"), axis=0),
                out_rows,
                preferred_element_type=jnp.float32,
            ).astype(jnp.bfloat16),
            "mp",
            0,
        )
        own_tokens = lax.dynamic_slice_in_dim(tokens, position * rows_own, rows_own, 0)
        residual = own_tokens.astype(jnp.float32) + attention_rows
        normed_own = layer_norm(residual, ln2_gain).astype(jnp.bfloat16)
        hidden = jax.nn.gelu(
            jnp.dot(
                gathered_copies(normed_own, "mp", 0), up_cols, preferred_element_type=jnp.float32
            ),
            approximate=False,
        ).astype(jnp.bfloat16)
        output = residual + lax.psum_scatter(
            jnp.dot(
                lax.slice_in_dim(hidden, 0, lax.axis_size("mp") * rows_own, axis=0),
                down_rows,
                preferred_element_type=jnp.float32,
            ).astype(jnp.bfloat16),
            "mp",
            scatter_dimension=0,
            tiled=True,
        ).astype(jnp.float32)
        wanted = lax.dynamic_index_in_dim(targets[0], slot, 0, keepdims=False).astype(jnp.float32)
        row_ids = position * rows_own + jnp.arange(rows_own, dtype=jnp.int32)
        kept_rows = row_ids < length
        misfit = output - wanted
        squares_run = squares_run + jnp.sum(jnp.where(kept_rows[:, None], misfit * misfit, 0.0))
        number_run = number_run + jnp.sum(kept_rows.astype(jnp.float32))
        stored = lax.dynamic_update_index_in_dim(stored, output.astype(jnp.bfloat16), slot, 0)
        return (stored, squares_run, number_run)

    start_state = (
        jnp.zeros((group_size, rows_own, D), jnp.bfloat16),
        jnp.zeros((), jnp.float32),
        jnp.zeros((), jnp.float32),
    )
    encoded, squares, number = lax.fori_loop(0, group_size, step, start_state)
    total_squares, total_number = (by_axis(squares, DP_MP), by_axis(number, DP_MP))
    return (encoded[None], total_squares / (D * total_number))


def solution(mesh):
    split = Mesh(mesh.devices.reshape(4, 4, 4, mesh.shape["mp"]), ("dp_0", "dp_1", "dp_2", "mp"))
    return jax.shard_map(
        on_device,
        mesh=split,
        in_specs=(
            P(DP_MP, None, None),
            P(DP, None),
            P(DP, None),
            P(DP, "mp"),
            P(None, DP, "mp"),
            P("mp", DP),
            P(DP, "mp"),
            P("mp", DP),
            P(),
            P(),
            P(DP, None, "mp", None),
        ),
        out_specs=(P(DP, None, "mp", None), P()),
        check_vma=False,
    )
```

profile of v0, /device:TPU:1, one launch (start us, length us, event | category | flops | bytes accessed | tf_op | source)
XLA Modules:
  0.0 418.0 jit_solution(11098841160835899786)
XLA Ops:
  11.9 70.7 %all-gather.7.cloned.1.call-done = bf16[2490368]{0:T(1024)(128)(2,1)} async-done(((bf16[38912]{0:T(1024)(128)(2,1)}), bf16[2490368]{0:T(1024)(128)(2,1)}) %all-gather.7.cloned.1.call-update) | async-done | bytes 4980752 | tf_op jit(solution)/shard_map/all_gather | solution.py:21
  82.6 7.8 %reshape.169 = bf16[64,38912]{1,0:T(8,128)(2,1)} reshape(bf16[2490368]{0:T(1024)(128)(2,1)} %all-gather.7.cloned.1.call-done) | data formatting | bytes 9961472 | tf_op jit(solution)/shard_map/all_gather | solution.py:21
  90.4 4.5 %slice.91 = bf16[64,32768]{1,0:T(8,128)(2,1)} slice(bf16[64,38912]{1,0:T(8,128)(2,1)} %reshape.169), slice={[0:64], [6144:38912]} | slice | bytes 8388608 | tf_op jit(solution)/shard_map/slice | solution.py:23
  94.9 7.5 %reshape_reshape.7 = bf16[1024,2048]{1,0:T(8,128)(2,1)} reshape(bf16[64,32768]{1,0:T(8,128)(2,1)} %slice.91) | data formatting | bytes 8388608 | tf_op jit(solution)/shard_map/reshape;reshape | solution.py:16
  104.3 58.3 %all-gather.5.cloned.1.call-done = bf16[1024,4096]{1,0:T(8,128)(2,1)} async-done(((bf16[16,4096]{1,0:T(8,128)(2,1)}), bf16[1024,4096]{1,0:T(8,128)(2,1)}) %all-gather.5.cloned.1.call-update) | async-done | bytes 8388624 | tf_op jit(solution)/shard_map/all_gather | solution.py:32
  162.6 4.7 %slice_bitcast_fusion = bf16[2048,1024]{0,1:T(8,128)(2,1)} fusion(bf16[1024,4096]{1,0:T(8,128)(2,1)} %all-gather.5.cloned.1.call-done), kind=kLoop, calls=%fused_computation.154 | loop fusion | bytes 8388608 | tf_op jit(solution)/shard_map/transpose | solution.py:35
  167.3 6.4 %copy.34 = bf16[2048,1024]{1,0:T(8,128)(2,1)} copy(bf16[2048,1024]{0,1:T(8,128)(2,1)} %slice_bitcast_fusion) | data formatting | bytes 8388608
  175.6 2.9 copy.35
  181.2 189.8 %while.61 = (s32[]{:T(128)}, bf16[2,256,1024]{2,1,0:T(8,128)(2,1)}, f32[]{:T(128)}, f32[]{:T(128)}, bf16[1,512,768]{2,1,0:T(8,128)(2,1)}, /*index=5*/s32[2]{0:T(...) while((s32[]{:T(128)}, bf16[2,256,1024]{2,1,0:T(8,128)(2,1)}, ...), condition=%wide.region_30.31_spmd.clone, body=%wide.region_0.30_spmd.clone.sunk | while | flops 6996395008 | bytes 102745624 | solution.py:199
  187.4 9.2 %all-gather.9.cloned.1.call-done = bf16[2,512,768]{2,1,0:T(8,128)(2,1)} async-done(((bf16[1,512,768]{2,1,0:T(8,128)(2,1)}), bf16[2,512,768]{2,1,0:T(8,128)(2,1)}) %all-gather.9.cloned.1.call-update) | async-done | bytes 1572880 | tf_op jit(solution)/shard_map/while/body/eval_jaxpr/all_gather | solution.py:41
  198.4 4.7 %all_to_all.45 = bf16[2,512,512]{2,1,0:T(8,128)(2,1)S(1)} all-to-all(bf16[2,512,512]{2,1,0:T(8,128)(2,1)S(1)} %broadcast_in_dim.226), channel_id=1, replica_groups=mesh['dp_0'=4,'dp_1'=4,'dp_2'=4,'mp'=2] {'mp'}, dimensions={0} | all-to-all | bytes 2097152 | tf_op jit(solution)/shard_map/while/body/eval_jaxpr/all_to_all | solution.py:46
  203.9 3.7 fusion.186
  212.3 11.5 %conditional.3 = (bf16[8,512,64]{1,2,0:T(8,128)(2,1)}) conditional(s32[]{:T(128)} %clamp.13, (bf16[8,512,64]{2,1,0:T(8,128)(2,1)S(1)}, bf16[8,512,64]{2,1,0:T(8,128)(2,1)S(1)}, pred[512]{0:T(512)(128)(4,1)S(1)}, bf16[8,512,64]{2,1,0:T(8,128)(2,1)S(1)}) %tuple.173, (bf16[8,512,64]{2,1,0:T(8,128)(2,1)S(1)}, ...), branch_computations={%region_4.8_spmd, %region_9.13_spmd, %region_14.18_spmd, %region_1... | conditional | flops 68713472 | bytes 6501041 | solution.py:105
  212.4 11.5 %while.60 = (s32[]{:T(128)}, bf16[8,512,64]{1,2,0:T(8,128)(2,1)}, pred[512]{0:T(512)(128)(4,1)S(1)}, bf16[8,512,64]{2,1,0:T(8,128)(2,1)S(1)}, bf16[8,512,64]{2,1...) while((s32[]{:T(128)}, bf16[8,512,64]{1,2,0:T(8,128)(2,1)}, ...), condition=%wide.region_23.22_spmd, body=%wide.region_20.21_spmd.sunk | while | flops 68713472 | bytes 3682893 | solution.py:91
  223.8 2.2 convolution_convert_fusion.5
  226.0 4.6 %all_to_all.46 = bf16[2,256,1024]{2,1,0:T(8,128)(2,1)S(1)} all-to-all(bf16[2,256,1024]{2,1,0:T(8,128)(2,1)S(1)} %bitcast.229), channel_id=1, replica_groups=mesh['dp_0'=4,'dp_1'=4,'dp_2'=4,'mp'=2] {'mp'}, dimensions={0} | all-to-all | bytes 2097152 | tf_op jit(solution)/shard_map/while/body/eval_jaxpr/all_to_all | solution.py:62
  231.7 4.6 %all_to_all.47 = bf16[2,256,1024]{2,1,0:T(8,128)(2,1)S(1)} all-to-all(bf16[2,256,1024]{2,1,0:T(8,128)(2,1)S(1)} %broadcast_in_dim.227), channel_id=1, replica_groups=mesh['dp_0'=4,'dp_1'=4,'dp_2'=4,'mp'=2] {'mp'}, dimensions={0} | all-to-all | bytes 2097152 | tf_op jit(solution)/shard_map/while/body/eval_jaxpr/all_to_all | solution.py:46
  236.2 16.4 %fusion.190 = bf16[512,1024]{1,0:T(8,128)(2,1)} fusion(bf16[2048,1024]{1,0:T(8,128)(2,1)} %get-tuple-element.1257, bf16[512,1024]{1,0:T(8,128)(2,1)S(1)} %bitcast.230, bf16[1024,2048]{1,0:T(8,128)(2,1)} %get-tuple-element.1256), kind=kOutput, calls=%fused_computation.92.clone.1 | convolution fusion | flops 4363649024 | bytes 10485760 | tf_op jit(solution)/shard_map/while/body/eval_jaxpr/dot_general | solution.py:176
  254.8 16.1 %reduce-scatter.2.cloned.1.call-done = bf16[256,1024]{1,0:T(8,128)(2,1)} async-done(((bf16[512,1024]{1,0:T(8,128)(2,1)}), bf16[256,1024]{1,0:T(8,128)(2,1)}) %reduce-scatter.2.cloned.1.call-update) | async-done | bytes 524304 | tf_op jit(solution)/shard_map/while/body/eval_jaxpr/reduce_scatter | solution.py:175
  281.5 10.3 %all-gather.9.cloned.1.call-done = bf16[2,512,768]{2,1,0:T(8,128)(2,1)} async-done(((bf16[1,512,768]{2,1,0:T(8,128)(2,1)}), bf16[2,512,768]{2,1,0:T(8,128)(2,1)}) %all-gather.9.cloned.1.call-update) | async-done | bytes 1572880 | tf_op jit(solution)/shard_map/while/body/eval_jaxpr/all_gather | solution.py:41
  293.6 4.7 %all_to_all.45 = bf16[2,512,512]{2,1,0:T(8,128)(2,1)S(1)} all-to-all(bf16[2,512,512]{2,1,0:T(8,128)(2,1)S(1)} %broadcast_in_dim.226), channel_id=1, replica_groups=mesh['dp_0'=4,'dp_1'=4,'dp_2'=4,'mp'=2] {'mp'}, dimensions={0} | all-to-all | bytes 2097152 | tf_op jit(solution)/shard_map/while/body/eval_jaxpr/all_to_all | solution.py:46
  299.1 3.7 fusion.186
  307.6 11.5 %conditional.3 = (bf16[8,512,64]{1,2,0:T(8,128)(2,1)}) conditional(s32[]{:T(128)} %clamp.13, (bf16[8,512,64]{2,1,0:T(8,128)(2,1)S(1)}, bf16[8,512,64]{2,1,0:T(8,128)(2,1)S(1)}, pred[512]{0:T(512)(128)(4,1)S(1)}, bf16[8,512,64]{2,1,0:T(8,128)(2,1)S(1)}) %tuple.173, (bf16[8,512,64]{2,1,0:T(8,128)(2,1)S(1)}, ...), branch_computations={%region_4.8_spmd, %region_9.13_spmd, %region_14.18_spmd, %region_1... | conditional | flops 68713472 | bytes 6501041 | solution.py:105
  307.6 11.5 %while.60 = (s32[]{:T(128)}, bf16[8,512,64]{1,2,0:T(8,128)(2,1)}, pred[512]{0:T(512)(128)(4,1)S(1)}, bf16[8,512,64]{2,1,0:T(8,128)(2,1)S(1)}, bf16[8,512,64]{2,1...) while((s32[]{:T(128)}, bf16[8,512,64]{1,2,0:T(8,128)(2,1)}, ...), condition=%wide.region_23.22_spmd, body=%wide.region_20.21_spmd.sunk | while | flops 68713472 | bytes 3682893 | solution.py:91
  321.3 4.6 %all_to_all.46 = bf16[2,256,1024]{2,1,0:T(8,128)(2,1)S(1)} all-to-all(bf16[2,256,1024]{2,1,0:T(8,128)(2,1)S(1)} %bitcast.229), channel_id=1, replica_groups=mesh['dp_0'=4,'dp_1'=4,'dp_2'=4,'mp'=2] {'mp'}, dimensions={0} | all-to-all | bytes 2097152 | tf_op jit(solution)/shard_map/while/body/eval_jaxpr/all_to_all | solution.py:62
  326.9 4.6 %all_to_all.47 = bf16[2,256,1024]{2,1,0:T(8,128)(2,1)S(1)} all-to-all(bf16[2,256,1024]{2,1,0:T(8,128)(2,1)S(1)} %broadcast_in_dim.227), channel_id=1, replica_groups=mesh['dp_0'=4,'dp_1'=4,'dp_2'=4,'mp'=2] {'mp'}, dimensions={0} | all-to-all | bytes 2097152 | tf_op jit(solution)/shard_map/while/body/eval_jaxpr/all_to_all | solution.py:46
  331.5 16.4 %fusion.190 = bf16[512,1024]{1,0:T(8,128)(2,1)} fusion(bf16[2048,1024]{1,0:T(8,128)(2,1)} %get-tuple-element.1257, bf16[512,1024]{1,0:T(8,128)(2,1)S(1)} %bitcast.230, bf16[1024,2048]{1,0:T(8,128)(2,1)} %get-tuple-element.1256), kind=kOutput, calls=%fused_computation.92.clone.1 | convolution fusion | flops 4363649024 | bytes 10485760 | tf_op jit(solution)/shard_map/while/body/eval_jaxpr/dot_general | solution.py:176
  350.0 16.2 %reduce-scatter.2.cloned.1.call-done = bf16[256,1024]{1,0:T(8,128)(2,1)} async-done(((bf16[512,1024]{1,0:T(8,128)(2,1)}), bf16[256,1024]{1,0:T(8,128)(2,1)}) %reduce-scatter.2.cloned.1.call-update) | async-done | bytes 524304 | tf_op jit(solution)/shard_map/while/body/eval_jaxpr/reduce_scatter | solution.py:175
  371.1 10.5 %all-reduce.2 = (f32[]{:T(128)}, f32[]{:T(128)}) all-reduce(f32[]{:T(128)} %get-tuple-element.1279, f32[]{:T(128)} %get-tuple-element.1280), channel_id=1, replica_groups=mesh['dp_0'=4,'dp_1'=4,'dp_2'=4,'mp'=2] {'dp_0'}, use_global_device_ids=true, to_apply=%region_31.32 | all-reduce | flops 2 | bytes 16 | tf_op jit(solution)/shard_map/psum | solution.py:68
  381.6 9.1 %all-reduce.1 = (f32[]{:T(128)}, f32[]{:T(128)}) all-reduce(f32[]{:T(128)} %get-tuple-element.808, f32[]{:T(128)} %get-tuple-element.809), channel_id=1, replica_groups=mesh['dp_0'=4,'dp_1'=4,'dp_2'=4,'mp'=2] {'dp_1'}, use_global_device_ids=true, to_apply=%region_32.33 | all-reduce | flops 2 | bytes 16 | tf_op jit(solution)/shard_map/psum | solution.py:68
  390.6 9.1 %all-reduce = (f32[]{:T(128)}, f32[]{:T(128)}) all-reduce(f32[]{:T(128)} %get-tuple-element.806, f32[]{:T(128)} %get-tuple-element.807), channel_id=1, replica_groups=mesh['dp_0'=4,'dp_1'=4,'dp_2'=4,'mp'=2] {'dp_2'}, use_global_device_ids=true, to_apply=%region_33.34 | all-reduce | flops 2 | bytes 16 | tf_op jit(solution)/shard_map/psum | solution.py:68
  399.7 9.1 %all-reduce.3 = (f32[]{:T(128)}, f32[]{:T(128)}) all-reduce(f32[]{:T(128)} %get-tuple-element.804, f32[]{:T(128)} %get-tuple-element.805), channel_id=1, replica_groups=mesh['dp_0'=4,'dp_1'=4,'dp_2'=4,'mp'=2] {'mp'}, use_global_device_ids=true, to_apply=%region_34.35 | all-reduce | flops 2 | bytes 16 | tf_op jit(solution)/shard_map/psum | solution.py:68
  (156 shorter events, 70.2 us)
Async XLA Ops:
  7.2 75.4 %all-gather.7.cloned.1.call-start = ((), (), s32[]{:S(2)}) async-start(), calls=%async_computation.5 | async-start | bytes 5058560 | tf_op jit(solution)/shard_map/all_gather | solution.py:21
  9.5 153.1 %all-gather.5.cloned.1.call-start = ((), (), s32[]{:S(2)}) async-start(), calls=%async_computation.4 | async-start | bytes 8519680 | tf_op jit(solution)/shard_map/all_gather | solution.py:32
  94.9 7.5 %slice-start = ((bf16[64,38912]{1,0:T(8,128)(2,1)}), bf16[64,6144]{1,0:T(8,128)(2,1)S(1)}, s32[]{:S(2)}) async-start(bf16[64,38912]{1,0:T(8,128)(2,1)} %reshape.169), calls=%async_computation.8 | async-start | bytes 1572864 | tf_op jit(solution)/shard_map/slice | solution.py:23
  173.7 1.9 slice-start.1
  175.6 5.6 %copy-start.6 = (f32[1024]{0:T(1024)S(1)}, f32[1024]{0:T(1024)}, u32[]{:S(2)}) copy-start(f32[1024]{0:T(1024)} %param.34) | copy-start | bytes 12292
  175.6 5.6 %copy-start.8 = (f32[1024]{0:T(1024)S(1)}, f32[1024]{0:T(1024)}, u32[]{:S(2)}) copy-start(f32[1024]{0:T(1024)} %param.33) | copy-start | bytes 12292
  175.6 5.6 %copy-start.9 = (s32[1,2]{1,0:T(1,128)S(1)}, s32[1,2]{1,0:T(1,128)}, u32[]{:S(2)}) copy-start(s32[1,2]{1,0:T(1,128)} %param.27) | copy-start | bytes 28
  175.6 5.6 %copy-start.10 = (s32[1,2]{1,0:T(1,128)S(1)}, s32[1,2]{1,0:T(1,128)}, u32[]{:S(2)}) copy-start(s32[1,2]{1,0:T(1,128)} %param.26) | copy-start | bytes 28
  178.5 2.7 copy-start.4
  181.4 15.2 %all-gather.9.cloned.1.call-start = ((), (), s32[]{:S(2)}) async-start(), calls=%async_computation.6 | async-start | bytes 2359296 | tf_op jit(solution)/shard_map/while/body/eval_jaxpr/all_gather | solution.py:41
  182.2 88.7 %reduce-scatter.2.cloned.1.call-start = ((), (), s32[]{:S(2)}) async-start(), calls=%async_computation.7 | async-start | bytes 1572864 | tf_op jit(solution)/shard_map/while/body/eval_jaxpr/reduce_scatter | solution.py:175
  198.3 5.6 %copy-start.3 = (bf16[3,1024,512]{1,2,0:T(8,128)(2,1)S(1)}, bf16[3,1024,512]{1,2,0:T(8,128)(2,1)}, u32[]{:S(2)}) copy-start(bf16[3,1024,512]{1,2,0:T(8,128)(2,1)} %get-tuple-element.1253) | copy-start | bytes 9437188 | tf_op jit(solution)/shard_map/while
  203.9 3.7 copy-start
  223.8 7.0 %copy-start.1 = (bf16[2,64,8,512]{3,2,0,1:T(8,128)(2,1)S(1)}, bf16[2,64,8,512]{3,2,0,1:T(8,128)(2,1)}, u32[]{:S(2)}) copy-start(bf16[2,64,8,512]{3,2,0,1:T(8,128)(2,1)} %copy-done) | copy-start | bytes 3145732 | tf_op jit(solution)/shard_map/while
  236.2 34.7 %copy-start.2 = (bf16[1,2,256,1024]{3,2,1,0:T(8,128)(2,1)S(1)}, bf16[1,2,256,1024]{3,2,1,0:T(8,128)(2,1)}, u32[]{:S(2)}) copy-start(bf16[1,2,256,1024]{3,2,1,0:T(8,128)(2,1)} %get-tuple-element.1259) | copy-start | bytes 3145732 | tf_op jit(solution)/shard_map/while
  252.7 23.1 %copy-start.5 = (bf16[768,512]{1,0:T(8,128)(2,1)S(1)}, bf16[768,512]{1,0:T(8,128)(2,1)}, u32[]{:S(2)}) copy-start(bf16[768,512]{1,0:T(8,128)(2,1)} %get-tuple-element.1301) | copy-start | bytes 2359300 | tf_op jit(solution)/shard_map/while
  275.8 16.1 %all-gather.9.cloned.1.call-start = ((), (), s32[]{:S(2)}) async-start(), calls=%async_computation.6 | async-start | bytes 2359296 | tf_op jit(solution)/shard_map/while/body/eval_jaxpr/all_gather | solution.py:41
  276.3 89.9 %reduce-scatter.2.cloned.1.call-start = ((), (), s32[]{:S(2)}) async-start(), calls=%async_computation.7 | async-start | bytes 1572864 | tf_op jit(solution)/shard_map/while/body/eval_jaxpr/reduce_scatter | solution.py:175
  293.6 5.6 %copy-start.3 = (bf16[3,1024,512]{1,2,0:T(8,128)(2,1)S(1)}, bf16[3,1024,512]{1,2,0:T(8,128)(2,1)}, u32[]{:S(2)}) copy-start(bf16[3,1024,512]{1,2,0:T(8,128)(2,1)} %get-tuple-element.1253) | copy-start | bytes 9437188 | tf_op jit(solution)/shard_map/while
  299.1 3.7 copy-start
  319.1 7.0 %copy-start.1 = (bf16[2,64,8,512]{3,2,0,1:T(8,128)(2,1)S(1)}, bf16[2,64,8,512]{3,2,0,1:T(8,128)(2,1)}, u32[]{:S(2)}) copy-start(bf16[2,64,8,512]{3,2,0,1:T(8,128)(2,1)} %copy-done) | copy-start | bytes 3145732 | tf_op jit(solution)/shard_map/while
  331.5 34.8 %copy-start.2 = (bf16[1,2,256,1024]{3,2,1,0:T(8,128)(2,1)S(1)}, bf16[1,2,256,1024]{3,2,1,0:T(8,128)(2,1)}, u32[]{:S(2)}) copy-start(bf16[1,2,256,1024]{3,2,1,0:T(8,128)(2,1)} %get-tuple-element.1259) | copy-start | bytes 3145732 | tf_op jit(solution)/shard_map/while
  347.9 23.2 %copy-start.5 = (bf16[768,512]{1,0:T(8,128)(2,1)S(1)}, bf16[768,512]{1,0:T(8,128)(2,1)}, u32[]{:S(2)}) copy-start(bf16[768,512]{1,0:T(8,128)(2,1)} %get-tuple-element.1301) | copy-start | bytes 2359300 | tf_op jit(solution)/shard_map/while
Sparse Core Ops, SparseCore 0:
  10.7 71.7 all-gather.6
  85.5 77.0 all-gather.4
  183.9 12.6 all-gather.8
  252.8 18.0 reduce-scatter.1
  277.9 13.9 all-gather.8
  348.1 18.1 reduce-scatter.1
where the time goes:
time: 421 us; the launch traced here: 418 us
  waiting for transfers between devices  182 us (43%)
  matrix products  67.8 us (16%)
  blocking collectives  65.4 us (16%)
  local copies, waits for them, and re-layouts  49.7 us (12%)
  other arithmetic  27.5 us (7%)
  between operations  16.4 us (4%)
  loops' own time  8.66 us (2%)
    all_gather x1, waiting for transfers between devices, one_gather(): lines, at, finished = (lax.all_gather(line, axis), 0, [])  70.7 us
    all_gather x1, waiting for transfers between devices, rows_first(): lax.all_gather(both, axis, axis=0, tiled=True)  58.3 us
    psum x4, blocking collectives, by_axis(): shard = lax.psum(shard, axis)  37.7 us
    dot_general x2, matrix products, step(): jnp.dot(lax.slice_in_dim(hidden, 0, lax.axis_size('mp') * rows_own, axis=...  32.9 us
    reduce_scatter x2, waiting for transfers between devices, step(): lax.psum_scatter(jnp.dot(lax.slice_in_dim(hidden, 0, lax.axis_size('mp')...  32.4 us
    all_gather x2, waiting for transfers between devices, broadcast(): lax.all_gather(shard, axis)  19.6 us
    all_to_all x4, blocking collectives, copy_for_each(): lax.all_to_all(jnp.broadcast_to(shard[None], (length, *shard.shape)), axi...  18.5 us
    dot_general x16, matrix products, one_head(): jnp.dot(expo.astype(jnp.bfloat16), value_part, preferred_element_type=jnp...  14.6 us
  transfers between devices with their start and end apart: 6, of which 6 were waited for; matrix products, arithmetic and copies ran while one was open for 8% of the time, Pallas kernels for 0%

commit v1 on v0

--- a/solution.py
+++ b/solution.py
@@ -8,6 +8,13 @@
 HEAD = 64
 DP = ("dp_0", "dp_1", "dp_2")
 DP_MP = ("dp_0", "dp_1", "dp_2", "mp")
+
+
+def all_by_exchange(block, mesh_axis, dim):
+    devices = lax.axis_size(mesh_axis)
+    blocks = jnp.stack([block for _ in range(devices)])
+    blocks = lax.all_to_all(blocks, mesh_axis, split_axis=0, concat_axis=0)
+    return jnp.concatenate(blocks, axis=dim)
 
 
 def joined_along(tiles, dim):
@@ -29,7 +36,7 @@
 def rows_first(arrays, axis, dims):
     turned = [jnp.moveaxis(a, dim, 0) for a, dim in zip(arrays, dims)]
     both = jnp.concatenate([t.reshape(len(t), -1) for t in turned], axis=1)
-    whole, at, finished = (lax.all_gather(both, axis, axis=0, tiled=True), 0, [])
+    whole, at, finished = (all_by_exchange(both, axis, 0), 0, [])
     for t, dim in zip(turned, dims):
         section = whole[:, at : at + t[0].size].reshape(-1, *t.shape[1:])
         finished.append(jnp.moveaxis(section, 0, dim))

time: 421 us -> 437 us (1.038)
  starting transfers between devices: 0.21 us -> 12.4 us
  local copies, waits for them, and re-layouts: 49.7 us -> 54.1 us
    all_to_all x0 -> x1, waiting for transfers between devices: none -> 118 us  [all_by_exchange(): blocks = lax.all_to_all(blocks, mesh_axis, split_axis=0, concat_axis=0)]
    all_gather x1 -> x0, waiting for transfers between devices: 58.3 us -> none  [rows_first(): lax.all_gather(both, axis, axis=0, tiled=True)]
    all_gather x1, waiting for transfers between devices: 70.7 us -> 12.4 us  [one_gather(): lines, at, finished = (lax.all_gather(line, axis), 0, [])]
    all_to_all x0 -> x1, starting transfers between devices: none -> 12.2 us  [all_by_exchange(): blocks = lax.all_to_all(blocks, mesh_axis, split_axis=0, concat_axis=0)]
    unnamed x14 -> x11, local copies, waits for them, and re-layouts: 11.5 us -> 8.62 us
  transfers between devices with their start and end apart: 6 -> 6, of which waited for: 6 -> 6; matrix products, arithmetic and copies ran while one was open for 8% -> 7% of each run, Pallas kernels for 0% -> 0%
where the time goes in v1:
time: 437 us; the launch traced here: 435 us
  waiting for transfers between devices  183 us (42%)
  matrix products  68.3 us (16%)
  blocking collectives  65.5 us (15%)
  local copies, waits for them, and re-layouts  54.1 us (12%)
  other arithmetic  26.7 us (6%)
  between operations  16.2 us (4%)
  starting transfers between devices  12.4 us (3%)
  loops' own time  8.57 us (2%)
    all_to_all x1, waiting for transfers between devices, all_by_exchange(): blocks = lax.all_to_all(blocks, mesh_axis, split_axis=0, concat_axis=0)  118 us
    psum x4, blocking collectives, by_axis(): shard = lax.psum(shard, axis)  37.8 us
    dot_general x2, matrix products, step(): jnp.dot(lax.slice_in_dim(hidden, 0, lax.axis_size('mp') * rows_own, axis=...  32.9 us
    reduce_scatter x2, waiting for transfers between devices, step(): lax.psum_scatter(jnp.dot(lax.slice_in_dim(hidden, 0, lax.axis_size('mp')...  32.5 us
    all_gather x2, waiting for transfers between devices, broadcast(): lax.all_gather(shard, axis)  18.7 us
    all_to_all x4, blocking collectives, copy_for_each(): lax.all_to_all(jnp.broadcast_to(shard[None], (length, *shard.shape)), axi...  18.5 us
    dot_general x16, matrix products, one_head(): jnp.dot(expo.astype(jnp.bfloat16), value_part, preferred_element_type=jnp...  14.7 us
    all_gather x1, waiting for transfers between devices, one_gather(): lines, at, finished = (lax.all_gather(line, axis), 0, [])  12.4 us
  transfers between devices with their start and end apart: 6, of which 6 were waited for; matrix products, arithmetic and copies ran while one was open for 7% of the time, Pallas kernels for 0%

profile of v1, /device:TPU:1, one launch (start us, length us, event | category | flops | bytes accessed | tf_op | source)
XLA Modules:
  0.0 434.8 jit_solution(11004374082741273283)
XLA Ops:
  11.1 4.3 stack.2
  15.4 12.2 %all-to-all-start.3 = ((bf16[64,16,4096]{2,1,0:T(8,128)(2,1)}), bf16[64,16,4096]{2,1,0:T(8,128)(2,1)}, u32[]{:S(2)}, u32[]{:S(2)}) async-start(bf16[64,16,4096]{2,1,0:T(8,128)(2,1)} %stack.2), calls=%async_computation.4 | async-start | bytes 16777216 | tf_op jit(solution)/shard_map/all_to_all | solution.py:16
  27.6 118.1 %all-to-all-done.3 = bf16[64,16,4096]{2,1,0:T(8,128)(2,1)} async-done(((bf16[64,16,4096]{2,1,0:T(8,128)(2,1)}), bf16[64,16,4096]{2,1,0:T(8,128)(2,1)}, u32[]{:S(2)}, u32[]{:S(2)}) %all-to-all-start.3) | async-done | bytes 8388640 | tf_op jit(solution)/shard_map/all_to_all | solution.py:16
  147.8 4.7 %slice_bitcast_fusion = bf16[2048,1024]{0,1:T(8,128)(2,1)} fusion(bf16[1024,4096]{1,0:T(8,128)(2,1)} %bitcast.21), kind=kLoop, calls=%fused_computation.154 | loop fusion | bytes 8388608 | tf_op jit(solution)/shard_map/transpose | solution.py:42
  152.6 6.4 %copy.39 = bf16[2048,1024]{1,0:T(8,128)(2,1)} copy(bf16[2048,1024]{0,1:T(8,128)(2,1)} %slice_bitcast_fusion) | data formatting | bytes 8388608
  164.5 12.4 %all-gather.4.cloned.1.call-done = bf16[2490368]{0:T(1024)(128)(2,1)} async-done(((bf16[38912]{0:T(1024)(128)(2,1)}), bf16[2490368]{0:T(1024)(128)(2,1)}) %all-gather.4.cloned.1.call-update) | async-done | bytes 4980752 | tf_op jit(solution)/shard_map/all_gather | solution.py:28
  176.9 7.8 %reshape.175 = bf16[64,38912]{1,0:T(8,128)(2,1)} reshape(bf16[2490368]{0:T(1024)(128)(2,1)} %all-gather.4.cloned.1.call-done) | data formatting | bytes 9961472 | tf_op jit(solution)/shard_map/all_gather | solution.py:28
  184.8 4.5 %slice.91 = bf16[64,32768]{1,0:T(8,128)(2,1)} slice(bf16[64,38912]{1,0:T(8,128)(2,1)} %reshape.175), slice={[0:64], [6144:38912]} | slice | bytes 8388608 | tf_op jit(solution)/shard_map/slice | solution.py:30
  189.3 7.5 %reshape_reshape.7 = bf16[1024,2048]{1,0:T(8,128)(2,1)} reshape(bf16[64,32768]{1,0:T(8,128)(2,1)} %slice.91) | data formatting | bytes 8388608 | tf_op jit(solution)/shard_map/reshape;reshape | solution.py:23
  198.6 189.3 %while.61 = (s32[]{:T(128)}, bf16[2,256,1024]{2,1,0:T(8,128)(2,1)}, f32[]{:T(128)}, f32[]{:T(128)}, bf16[1,512,768]{2,1,0:T(8,128)(2,1)}, /*index=5*/s32[2]{0:T(...) while((s32[]{:T(128)}, bf16[2,256,1024]{2,1,0:T(8,128)(2,1)}, ...), condition=%wide.region_30.31_spmd.clone, body=%wide.region_0.30_spmd.clone.sunk | while | flops 6996395008 | bytes 99599864 | solution.py:206
  204.8 8.4 %all-gather.6.cloned.1.call-done = bf16[2,512,768]{2,1,0:T(8,128)(2,1)} async-done(((bf16[1,512,768]{2,1,0:T(8,128)(2,1)}), bf16[2,512,768]{2,1,0:T(8,128)(2,1)}) %all-gather.6.cloned.1.call-update) | async-done | bytes 1572880 | tf_op jit(solution)/shard_map/while/body/eval_jaxpr/all_gather | solution.py:48
  215.2 4.7 %all_to_all.50 = bf16[2,512,512]{2,1,0:T(8,128)(2,1)S(1)} all-to-all(bf16[2,512,512]{2,1,0:T(8,128)(2,1)S(1)} %broadcast_in_dim.226), channel_id=1, replica_groups=mesh['dp_0'=4,'dp_1'=4,'dp_2'=4,'mp'=2] {'mp'}, dimensions={0} | all-to-all | bytes 2097152 | tf_op jit(solution)/shard_map/while/body/eval_jaxpr/all_to_all | solution.py:53
  220.7 3.7 fusion.186
  229.1 11.6 %conditional.3 = (bf16[8,512,64]{1,2,0:T(8,128)(2,1)}) conditional(s32[]{:T(128)} %clamp.13, (bf16[8,512,64]{2,1,0:T(8,128)(2,1)S(1)}, bf16[8,512,64]{2,1,0:T(8,128)(2,1)S(1)}, pred[512]{0:T(512)(128)(4,1)S(1)}, bf16[8,512,64]{2,1,0:T(8,128)(2,1)S(1)}) %tuple.172, (bf16[8,512,64]{2,1,0:T(8,128)(2,1)S(1)}, ...), branch_computations={%region_4.8_spmd, %region_9.13_spmd, %region_14.18_spmd, %region_1... | conditional | flops 68713472 | bytes 6501041 | solution.py:112
  229.1 11.5 %while.60 = (s32[]{:T(128)}, bf16[8,512,64]{1,2,0:T(8,128)(2,1)}, pred[512]{0:T(512)(128)(4,1)S(1)}, bf16[8,512,64]{2,1,0:T(8,128)(2,1)S(1)}, bf16[8,512,64]{2,1...) while((s32[]{:T(128)}, bf16[8,512,64]{1,2,0:T(8,128)(2,1)}, ...), condition=%wide.region_23.22_spmd, body=%wide.region_20.21_spmd.sunk | while | flops 68713472 | bytes 3682893 | solution.py:98
  242.9 4.6 %all_to_all.51 = bf16[2,256,1024]{2,1,0:T(8,128)(2,1)S(1)} all-to-all(bf16[2,256,1024]{2,1,0:T(8,128)(2,1)S(1)} %bitcast.230), channel_id=1, replica_groups=mesh['dp_0'=4,'dp_1'=4,'dp_2'=4,'mp'=2] {'mp'}, dimensions={0} | all-to-all | bytes 2097152 | tf_op jit(solution)/shard_map/while/body/eval_jaxpr/all_to_all | solution.py:69
  248.5 4.6 %all_to_all.52 = bf16[2,256,1024]{2,1,0:T(8,128)(2,1)S(1)} all-to-all(bf16[2,256,1024]{2,1,0:T(8,128)(2,1)S(1)} %broadcast_in_dim.227), channel_id=1, replica_groups=mesh['dp_0'=4,'dp_1'=4,'dp_2'=4,'mp'=2] {'mp'}, dimensions={0} | all-to-all | bytes 2097152 | tf_op jit(solution)/shard_map/while/body/eval_jaxpr/all_to_all | solution.py:53
  253.1 16.4 %fusion.190 = bf16[512,1024]{1,0:T(8,128)(2,1)} fusion(bf16[2048,1024]{1,0:T(8,128)(2,1)} %get-tuple-element.1274, bf16[512,1024]{1,0:T(8,128)(2,1)S(1)} %bitcast.231, bf16[1024,2048]{1,0:T(8,128)(2,1)} %get-tuple-element.1273), kind=kOutput, calls=%fused_computation.92.clone.1 | convolution fusion | flops 4363649024 | bytes 10485760 | tf_op jit(solution)/shard_map/while/body/eval_jaxpr/dot_general | solution.py:183
  271.5 16.2 %reduce-scatter.2.cloned.1.call-done = bf16[256,1024]{1,0:T(8,128)(2,1)} async-done(((bf16[512,1024]{1,0:T(8,128)(2,1)}), bf16[256,1024]{1,0:T(8,128)(2,1)}) %reduce-scatter.2.cloned.1.call-update) | async-done | bytes 524304 | tf_op jit(solution)/shard_map/while/body/eval_jaxpr/reduce_scatter | solution.py:182
  298.3 10.3 %all-gather.6.cloned.1.call-done = bf16[2,512,768]{2,1,0:T(8,128)(2,1)} async-done(((bf16[1,512,768]{2,1,0:T(8,128)(2,1)}), bf16[2,512,768]{2,1,0:T(8,128)(2,1)}) %all-gather.6.cloned.1.call-update) | async-done | bytes 1572880 | tf_op jit(solution)/shard_map/while/body/eval_jaxpr/all_gather | solution.py:48
  310.6 4.7 %all_to_all.50 = bf16[2,512,512]{2,1,0:T(8,128)(2,1)S(1)} all-to-all(bf16[2,512,512]{2,1,0:T(8,128)(2,1)S(1)} %broadcast_in_dim.226), channel_id=1, replica_groups=mesh['dp_0'=4,'dp_1'=4,'dp_2'=4,'mp'=2] {'mp'}, dimensions={0} | all-to-all | bytes 2097152 | tf_op jit(solution)/shard_map/while/body/eval_jaxpr/all_to_all | solution.py:53
  316.1 3.7 fusion.186
  324.5 11.6 %conditional.3 = (bf16[8,512,64]{1,2,0:T(8,128)(2,1)}) conditional(s32[]{:T(128)} %clamp.13, (bf16[8,512,64]{2,1,0:T(8,128)(2,1)S(1)}, bf16[8,512,64]{2,1,0:T(8,128)(2,1)S(1)}, pred[512]{0:T(512)(128)(4,1)S(1)}, bf16[8,512,64]{2,1,0:T(8,128)(2,1)S(1)}) %tuple.172, (bf16[8,512,64]{2,1,0:T(8,128)(2,1)S(1)}, ...), branch_computations={%region_4.8_spmd, %region_9.13_spmd, %region_14.18_spmd, %region_1... | conditional | flops 68713472 | bytes 6501041 | solution.py:112
  324.5 11.5 %while.60 = (s32[]{:T(128)}, bf16[8,512,64]{1,2,0:T(8,128)(2,1)}, pred[512]{0:T(512)(128)(4,1)S(1)}, bf16[8,512,64]{2,1,0:T(8,128)(2,1)S(1)}, bf16[8,512,64]{2,1...) while((s32[]{:T(128)}, bf16[8,512,64]{1,2,0:T(8,128)(2,1)}, ...), condition=%wide.region_23.22_spmd, body=%wide.region_20.21_spmd.sunk | while | flops 68713472 | bytes 3682893 | solution.py:98
  338.3 4.6 %all_to_all.51 = bf16[2,256,1024]{2,1,0:T(8,128)(2,1)S(1)} all-to-all(bf16[2,256,1024]{2,1,0:T(8,128)(2,1)S(1)} %bitcast.230), channel_id=1, replica_groups=mesh['dp_0'=4,'dp_1'=4,'dp_2'=4,'mp'=2] {'mp'}, dimensions={0} | all-to-all | bytes 2097152 | tf_op jit(solution)/shard_map/while/body/eval_jaxpr/all_to_all | solution.py:69
  343.9 4.6 %all_to_all.52 = bf16[2,256,1024]{2,1,0:T(8,128)(2,1)S(1)} all-to-all(bf16[2,256,1024]{2,1,0:T(8,128)(2,1)S(1)} %broadcast_in_dim.227), channel_id=1, replica_groups=mesh['dp_0'=4,'dp_1'=4,'dp_2'=4,'mp'=2] {'mp'}, dimensions={0} | all-to-all | bytes 2097152 | tf_op jit(solution)/shard_map/while/body/eval_jaxpr/all_to_all | solution.py:53
  348.4 16.4 %fusion.190 = bf16[512,1024]{1,0:T(8,128)(2,1)} fusion(bf16[2048,1024]{1,0:T(8,128)(2,1)} %get-tuple-element.1274, bf16[512,1024]{1,0:T(8,128)(2,1)S(1)} %bitcast.231, bf16[1024,2048]{1,0:T(8,128)(2,1)} %get-tuple-element.1273), kind=kOutput, calls=%fused_computation.92.clone.1 | convolution fusion | flops 4363649024 | bytes 10485760 | tf_op jit(solution)/shard_map/while/body/eval_jaxpr/dot_general | solution.py:183
  366.9 16.3 %reduce-scatter.2.cloned.1.call-done = bf16[256,1024]{1,0:T(8,128)(2,1)} async-done(((bf16[512,1024]{1,0:T(8,128)(2,1)}), bf16[256,1024]{1,0:T(8,128)(2,1)}) %reduce-scatter.2.cloned.1.call-update) | async-done | bytes 524304 | tf_op jit(solution)/shard_map/while/body/eval_jaxpr/reduce_scatter | solution.py:182
  387.9 10.5 %all-reduce.2 = (f32[]{:T(128)}, f32[]{:T(128)}) all-reduce(f32[]{:T(128)} %get-tuple-element.650, f32[]{:T(128)} %get-tuple-element.651), channel_id=1, replica_groups=mesh['dp_0'=4,'dp_1'=4,'dp_2'=4,'mp'=2] {'dp_0'}, use_global_device_ids=true, to_apply=%region_31.32 | all-reduce | flops 2 | bytes 16 | tf_op jit(solution)/shard_map/psum | solution.py:75
  398.5 9.1 %all-reduce.1 = (f32[]{:T(128)}, f32[]{:T(128)}) all-reduce(f32[]{:T(128)} %get-tuple-element.825, f32[]{:T(128)} %get-tuple-element.826), channel_id=1, replica_groups=mesh['dp_0'=4,'dp_1'=4,'dp_2'=4,'mp'=2] {'dp_1'}, use_global_device_ids=true, to_apply=%region_32.33 | all-reduce | flops 2 | bytes 16 | tf_op jit(solution)/shard_map/psum | solution.py:75
  407.6 9.0 %all-reduce = (f32[]{:T(128)}, f32[]{:T(128)}) all-reduce(f32[]{:T(128)} %get-tuple-element.823, f32[]{:T(128)} %get-tuple-element.824), channel_id=1, replica_groups=mesh['dp_0'=4,'dp_1'=4,'dp_2'=4,'mp'=2] {'dp_2'}, use_global_device_ids=true, to_apply=%region_33.34 | all-reduce | flops 2 | bytes 16 | tf_op jit(solution)/shard_map/psum | solution.py:75
  416.6 9.2 %all-reduce.3 = (f32[]{:T(128)}, f32[]{:T(128)}) all-reduce(f32[]{:T(128)} %get-tuple-element.821, f32[]{:T(128)} %get-tuple-element.822), channel_id=1, replica_groups=mesh['dp_0'=4,'dp_1'=4,'dp_2'=4,'mp'=2] {'mp'}, use_global_device_ids=true, to_apply=%region_34.35 | all-reduce | flops 2 | bytes 16 | tf_op jit(solution)/shard_map/psum | solution.py:75
  (149 shorter events, 75.1 us)
Async XLA Ops:
  7.2 169.8 %all-gather.4.cloned.1.call-start = ((), (), s32[]{:S(2)}) async-start(), calls=%async_computation.5 | async-start | bytes 5058560 | tf_op jit(solution)/shard_map/all_gather | solution.py:28
  15.4 130.4 %all-to-all-start.3 = ((bf16[64,16,4096]{2,1,0:T(8,128)(2,1)}), bf16[64,16,4096]{2,1,0:T(8,128)(2,1)}, u32[]{:S(2)}, u32[]{:S(2)}) async-start(bf16[64,16,4096]{2,1,0:T(8,128)(2,1)} %stack.2), calls=%async_computation.4 | async-start | bytes 16777216 | tf_op jit(solution)/shard_map/all_to_all | solution.py:16
  189.2 7.5 %slice-start = ((bf16[64,38912]{1,0:T(8,128)(2,1)}), bf16[64,6144]{1,0:T(8,128)(2,1)S(1)}, s32[]{:S(2)}) async-start(bf16[64,38912]{1,0:T(8,128)(2,1)} %reshape.175), calls=%async_computation.8 | async-start | bytes 1572864 | tf_op jit(solution)/shard_map/slice | solution.py:30
  189.2 9.4 %copy-start.4 = (f32[1024]{0:T(1024)S(1)}, f32[1024]{0:T(1024)}, u32[]{:S(2)}) copy-start(f32[1024]{0:T(1024)} %param.34) | copy-start | bytes 12292
  189.2 9.4 %copy-start.6 = (f32[1024]{0:T(1024)S(1)}, f32[1024]{0:T(1024)}, u32[]{:S(2)}) copy-start(f32[1024]{0:T(1024)} %param.33) | copy-start | bytes 12292
  189.2 9.4 %copy-start.7 = (s32[1,2]{1,0:T(1,128)S(1)}, s32[1,2]{1,0:T(1,128)}, u32[]{:S(2)}) copy-start(s32[1,2]{1,0:T(1,128)} %param.27) | copy-start | bytes 28
  189.3 9.4 %copy-start.8 = (s32[1,2]{1,0:T(1,128)S(1)}, s32[1,2]{1,0:T(1,128)}, u32[]{:S(2)}) copy-start(s32[1,2]{1,0:T(1,128)} %param.26) | copy-start | bytes 28
  198.8 14.3 %all-gather.6.cloned.1.call-start = ((), (), s32[]{:S(2)}) async-start(), calls=%async_computation.6 | async-start | bytes 2359296 | tf_op jit(solution)/shard_map/while/body/eval_jaxpr/all_gather | solution.py:48
  199.6 88.2 %reduce-scatter.2.cloned.1.call-start = ((), (), s32[]{:S(2)}) async-start(), calls=%async_computation.7 | async-start | bytes 1572864 | tf_op jit(solution)/shard_map/while/body/eval_jaxpr/reduce_scatter | solution.py:182
  215.1 5.6 %copy-start.3 = (bf16[3,1024,512]{1,2,0:T(8,128)(2,1)S(1)}, bf16[3,1024,512]{1,2,0:T(8,128)(2,1)}, u32[]{:S(2)}) copy-start(bf16[3,1024,512]{1,2,0:T(8,128)(2,1)} %get-tuple-element.1270) | copy-start | bytes 9437188 | tf_op jit(solution)/shard_map/while
  220.7 3.7 copy-start
  240.7 7.0 %copy-start.1 = (bf16[2,64,8,512]{3,2,0,1:T(8,128)(2,1)S(1)}, bf16[2,64,8,512]{3,2,0,1:T(8,128)(2,1)}, u32[]{:S(2)}) copy-start(bf16[2,64,8,512]{3,2,0,1:T(8,128)(2,1)} %copy-done) | copy-start | bytes 3145732 | tf_op jit(solution)/shard_map/while
  253.1 34.7 %copy-start.2 = (bf16[1,2,256,1024]{3,2,1,0:T(8,128)(2,1)S(1)}, bf16[1,2,256,1024]{3,2,1,0:T(8,128)(2,1)}, u32[]{:S(2)}) copy-start(bf16[1,2,256,1024]{3,2,1,0:T(8,128)(2,1)} %get-tuple-element.1276) | copy-start | bytes 3145732 | tf_op jit(solution)/shard_map/while
  292.5 16.1 %all-gather.6.cloned.1.call-start = ((), (), s32[]{:S(2)}) async-start(), calls=%async_computation.6 | async-start | bytes 2359296 | tf_op jit(solution)/shard_map/while/body/eval_jaxpr/all_gather | solution.py:48
  293.1 90.1 %reduce-scatter.2.cloned.1.call-start = ((), (), s32[]{:S(2)}) async-start(), calls=%async_computation.7 | async-start | bytes 1572864 | tf_op jit(solution)/shard_map/while/body/eval_jaxpr/reduce_scatter | solution.py:182
  310.5 5.6 %copy-start.3 = (bf16[3,1024,512]{1,2,0:T(8,128)(2,1)S(1)}, bf16[3,1024,512]{1,2,0:T(8,128)(2,1)}, u32[]{:S(2)}) copy-start(bf16[3,1024,512]{1,2,0:T(8,128)(2,1)} %get-tuple-element.1270) | copy-start | bytes 9437188 | tf_op jit(solution)/shard_map/while
  316.1 3.7 copy-start
  336.0 7.0 %copy-start.1 = (bf16[2,64,8,512]{3,2,0,1:T(8,128)(2,1)S(1)}, bf16[2,64,8,512]{3,2,0,1:T(8,128)(2,1)}, u32[]{:S(2)}) copy-start(bf16[2,64,8,512]{3,2,0,1:T(8,128)(2,1)} %copy-done) | copy-start | bytes 3145732 | tf_op jit(solution)/shard_map/while
  348.4 34.8 %copy-start.2 = (bf16[1,2,256,1024]{3,2,1,0:T(8,128)(2,1)S(1)}, bf16[1,2,256,1024]{3,2,1,0:T(8,128)(2,1)}, u32[]{:S(2)}) copy-start(bf16[1,2,256,1024]{3,2,1,0:T(8,128)(2,1)} %get-tuple-element.1276) | copy-start | bytes 3145732 | tf_op jit(solution)/shard_map/while
Sparse Core Ops, SparseCore 0:
  10.7 166.1 all-gather.3
  201.3 11.8 all-gather.5
  269.6 18.0 reduce-scatter.1
  294.6 13.8 all-gather.5
  365.0 18.1 reduce-scatter.1
